TPU v7x, 32 devices: a whole 2x2x4 slice. The times are simulated.
32 devices in a mesh: dp: 2 (over x), tp: 4 (over z), sp: 4 (over y, core).
Axes of the slice: x: 2, y: 2, z: 4, core: 2. Of those that a mesh axis runs over, the one named last changes fastest.
Arguments:
- tok_hidden: bfloat16 [512, 4096], P('dp'), parts along dimension 0
- cache_len: int32 [512], P('dp'), parts along dimension 0
- k_cache: bfloat16 [512, 32, 64, 128], P('dp', 'tp', 'sp'), parts along dimension 0
- v_cache: bfloat16 [512, 32, 64, 128], P('dp', 'tp', 'sp'), parts along dimension 0
- ln_gain: float32 [4096], replicated
- ln_bias: float32 [4096], replicated
- w_qkv: bfloat16 [4096, 3, 32, 128], P(None, None, 'tp')
- b_qkv: bfloat16 [3, 32, 128], P(None, 'tp')
- w_out: bfloat16 [32, 128, 4096], P('tp')
- b_out: bfloat16 [4096], replicated
Outputs:
- output 1: bfloat16 [512, 4096], P('dp'), parts along dimension 0
- output 2: bfloat16 [512, 32, 64, 128], P('dp', 'tp', 'sp'), parts along dimension 0
- output 3: bfloat16 [512, 32, 64, 128], P('dp', 'tp', 'sp'), parts along dimension 0
There are 2 independent parts. A program takes and returns all parts, laid end to end along the dimension named above; an argument that names none is the same for every part.
All inputs are finite; a program needn't handle non-finite values.
Results may differ from a plain program's by a relative error of at most 0.00849222.
Values sent between devices are 32-bit elements.
A program may use at most 1 GiB of HBM per device.

v0:
```python
import functools

import jax
import jax.numpy as jnp
from jax import lax
from jax.experimental import pallas as pl
from jax.experimental.pallas import tpu as pltpu
from jax.sharding import PartitionSpec as P

MESH = pl.DeviceIdType.MESH
NEG = float(jnp.finfo(jnp.float32).min)
F32 = jnp.float32
BF16 = jnp.bfloat16


def front_kernel(slots, mc, blk, len_hbm, x_hbm, gain_hbm, bias_hbm, w_hbm, bqkv_hbm, k_hbm, v_hbm,
                 ko_hbm, vo_hbm, k_buf, v_buf, qkv, len_ref, gain_ref, bias_ref, bqkv_ref, x_buf, hid, w_buf,
                 small_sem, x_sem, w_sem, k_sem, v_sem, ko_sem, vo_sem):
    rows, width = x_buf.shape
    heads, dim = qkv.shape[1], qkv.shape[3]
    ring = w_buf.shape[0]
    n_m = width // mc
    total = 3 * n_m
    n_blk = rows // blk
    first = lax.axis_index('sp') * slots

    def w_load(t, m, slot):
        return pltpu.make_async_copy(w_hbm.at[pl.ds(m * mc, mc), t], w_buf.at[slot], w_sem.at[slot])

    def cache_copies(i):
        part = pl.ds(i * blk, blk)
        return (pltpu.make_async_copy(k_hbm.at[part], k_buf.at[part], k_sem.at[i]),
                pltpu.make_async_copy(v_hbm.at[part], v_buf.at[part], v_sem.at[i]))

    def out_copies(i):
        part = pl.ds(i * blk, blk)
        return (pltpu.make_async_copy(k_buf.at[part], ko_hbm.at[part], ko_sem.at[i]),
                pltpu.make_async_copy(v_buf.at[part], vo_hbm.at[part], vo_sem.at[i]))

    load_x = pltpu.make_async_copy(x_hbm, x_buf, x_sem)
    load_x.start()
    small = [pltpu.make_async_copy(src, dst, small_sem.at[n]) for n, (src, dst) in enumerate(
        ((gain_hbm, gain_ref), (bias_hbm, bias_ref), (bqkv_hbm, bqkv_ref), (len_hbm, len_ref)))]
    for cp in small:
        cp.start()
    for c in range(ring):
        w_load(c // n_m, c % n_m, c).start()
    load_x.wait()
    for cp in small:
        cp.wait()

    @pl.loop(0, rows // LN_ROWS)
    def _(i):
        part = pl.ds(pl.multiple_of(i * LN_ROWS, LN_ROWS), LN_ROWS)
        x = x_buf[part].astype(F32)
        mean = jnp.mean(x, axis=-1, keepdims=True)
        centered = x - mean
        var = jnp.mean(centered * centered, axis=-1, keepdims=True)
        hid[part] = (centered * lax.rsqrt(var + 1e-5) * gain_ref[...] + bias_ref[...]).astype(BF16)
        per = n_blk // EARLY

        @pl.when(i < EARLY)
        def _():
            for u in range(per):
                for cp in cache_copies(i * per + u):
                    cp.start()

    @pl.loop(0, 3)
    def _(t):
        bias = bqkv_ref[t].astype(F32)
        for m in range(n_m):
            c = t * n_m + m
            slot = lax.rem(c, ring)
            w_load(t, m, slot).wait()
            w = jnp.swapaxes(w_buf[slot], 0, 1)
            for h in range(0, heads, 2):
                r = jnp.dot(hid[:, m * mc:(m + 1) * mc], jnp.concatenate([w[h], w[h + 1]], axis=1), preferred_element_type=F32)
                for u in range(2):
                    part = r[:, u * dim:(u + 1) * dim]
                    if m:
                        part = qkv[t, h + u] + part
                    if m == n_m - 1:
                        part = (part + bias[h + u:h + u + 1]).astype(BF16).astype(F32)
                    qkv[t, h + u] = part
            ahead = m + ring

            @pl.when(c + ring < total)
            def _():
                w_load(t + ahead // n_m, ahead % n_m, slot).start()

    slot_id = lax.broadcasted_iota(jnp.int32, (slots, dim), 0)

    @pl.loop(0, n_blk)
    def _(i):
        for cp in cache_copies(i):
            cp.wait()
        for b in range(blk):
            at = i * blk + b
            hit = (slot_id == len_ref[at] - first)[None]
            for t, buf in ((1, k_buf), (2, v_buf)):
                new = jnp.broadcast_to(qkv[t, :, pl.ds(at, 1), :], (heads, slots, dim)).astype(BF16)
                buf[at] = jnp.where(hit, new, buf[at])
        for cp in out_copies(i):
            cp.start()

    @pl.loop(0, n_blk)
    def _(i):
        for cp in out_copies(i):
            cp.wait()


LN_ROWS = 64
EARLY = 4


def in_hbm(*arrays):
    return [pltpu.with_memory_space_constraint(a, pltpu.HBM) for a in arrays]


def front(tok_hidden, cache_len, k_cache, v_cache, ln_gain, ln_bias, w_qkv, b_qkv, mc, ring, blk):
    rows, heads, slots, dim = k_cache.shape
    width = tok_hidden.shape[1]
    vmem = pl.BlockSpec(memory_space=pltpu.VMEM)
    hbm = pl.BlockSpec(memory_space=pltpu.HBM)
    dma = pltpu.SemaphoreType.DMA
    n_blk = rows // blk
    return pl.pallas_call(
        functools.partial(front_kernel, slots, mc, blk),
        in_specs=[hbm] * 8,
        out_specs=[hbm, hbm, vmem, vmem, vmem],
        out_shape=[
            jax.ShapeDtypeStruct(k_cache.shape, BF16),
            jax.ShapeDtypeStruct(v_cache.shape, BF16),
            pltpu.VMEM(k_cache.shape, BF16),
            pltpu.VMEM(v_cache.shape, BF16),
            pltpu.VMEM((3, heads, rows, dim), F32),
        ],
        scratch_shapes=[
            pltpu.SMEM((rows,), jnp.int32), pltpu.VMEM((1, width), F32), pltpu.VMEM((1, width), F32), pltpu.VMEM(b_qkv.shape, BF16),
            pltpu.VMEM((rows, width), BF16), pltpu.VMEM((rows, width), BF16),
            pltpu.VMEM((ring, mc, heads, dim), BF16),
            dma((4,)), dma, dma((ring,)), dma((n_blk,)), dma((n_blk,)), dma((n_blk,)), dma((n_blk,)),
        ],
        compiler_params=pltpu.CompilerParams(vmem_limit_bytes=34 * 2**20),
    )(*in_hbm(cache_len, tok_hidden, ln_gain.reshape(1, width), ln_bias.reshape(1, width), w_qkv, b_qkv, k_cache, v_cache))


def combine_kernel(quarter, rc, cc, len_hbm, qkv_ref, k_ref, v_ref, x_hbm, w_hbm, b_hbm, y_ref, len_ref, b_tiles, b_ref,
                   acc_ref, st_ref, scores, probs, got_acc, got_st, fwd_acc, fwd_st, own_acc, own_st, far_acc, far_st, att,
                   w_buf, x_buf, mine, near, half, far_half, tot, from_y, from_c, from_yc, load_sem, len_sem, b_sem,
                   a_s, a_r, as_s, as_r, b_s, b_r, bs_s, bs_r,
                   x_s, x_r, p_s, p_r, t_s, t_r, y_s, y_r, c_s, c_r, f_s, f_r):
    heads, slots, dim = k_ref.shape[1:]
    n_row, n_col = quarter // rc, w_hbm.shape[1] // cc
    n = n_row * n_col
    r = lax.axis_index('sp')
    z = lax.axis_index('tp')
    core, chip_y = lax.rem(r, 2), r // 2
    mate = {'sp': chip_y * 2 + (1 - core)}
    across = {'sp': (1 - chip_y) * 2 + core}
    outer = (z == 0) | (z == 3)
    inward = {'tp': jnp.where(z == 0, 1, 2)}
    outward = {'tp': jnp.where(z == 1, 0, 3)}
    peer = {'tp': 3 - z}

    load_len = pltpu.make_async_copy(len_hbm, len_ref, len_sem)
    load_len.start()
    load_b = pltpu.make_async_copy(b_hbm, b_tiles, b_sem)
    load_b.start()
    load_x = pltpu.make_async_copy(x_hbm, x_buf, load_sem.at[0])
    load_x.start()
    w_loads = []
    for j in range(n_col):
        cp = pltpu.make_async_copy(w_hbm.at[:, pl.ds(j * cc, cc)], w_buf.at[:, pl.ds(j * cc, cc)], load_sem.at[1 + j])
        cp.start()
        w_loads.append(cp)

    barrier = pltpu.get_barrier_semaphore()
    pl.semaphore_signal(barrier, inc=1, device_id=mate, device_id_type=MESH)
    pl.semaphore_signal(barrier, inc=1, device_id=across, device_id_type=MESH)

    @pl.when(outer)
    def _():
        pl.semaphore_signal(barrier, inc=1, device_id=inward, device_id_type=MESH)
        pl.semaphore_wait(barrier, 3)

    @pl.when(jnp.logical_not(outer))
    def _():
        pl.semaphore_signal(barrier, inc=1, device_id=outward, device_id_type=MESH)
        pl.semaphore_signal(barrier, inc=1, device_id=peer, device_id_type=MESH)
        pl.semaphore_wait(barrier, 4)

    def remote(src, dst, s, rcv, dev):
        return pltpu.make_async_remote_copy(src_ref=src, dst_ref=dst, send_sem=s, recv_sem=rcv, device_id=dev, device_id_type=MESH)

    mate_blocks = ((1 - chip_y) * 2 + (1 - core), chip_y * 2 + (1 - core))
    my_blocks = ((1 - chip_y) * 2 + core, chip_y * 2 + core)

    def a_stat(k, i):
        return remote(st_ref.at[i, mate_blocks[k]], got_st.at[k, i], as_s.at[k, i], as_r.at[k, i], mate)

    def a_copy(k, i):
        return remote(acc_ref.at[pl.ds(mate_blocks[k] * quarter + i * rc, rc)], got_acc.at[k, pl.ds(i * rc, rc)],
                      a_s.at[k, i], a_r.at[k, i], mate)

    load_len.wait()
    load_b.wait()
    bias = b_tiles[...].astype(F32)
    for j in range(bias.shape[0]):
        b_ref[:, j * 128:(j + 1) * 128] = bias[j:j + 1]
    lane = lax.broadcasted_iota(jnp.int32, (heads, 128), 1)

    def join(one, two):
        m_one, m_two = one, two
        top = jnp.maximum(m_one, m_two)
        f_one, f_two = jnp.exp(m_one - top), jnp.exp(m_two - top)
        l_one = pltpu.roll(one, 128 - quarter, 1)
        l_two = pltpu.roll(two, 128 - quarter, 1)
        total = l_one * f_one + l_two * f_two
        packed = jnp.where(lane < quarter, top, pltpu.roll(total, quarter, 1))
        return packed, f_one, f_two, total

    def b_stat(i):
        return remote(fwd_st.at[i], far_st.at[i], bs_s.at[i], bs_r.at[i], across)

    def b_copy(i):
        return remote(fwd_acc.at[pl.ds(i * rc, rc)], far_acc.at[pl.ds(i * rc, rc)], b_s.at[i], b_r.at[i], across)

    first = r * slots
    flat = heads * slots
    row_id = lax.broadcasted_iota(jnp.int32, (heads, flat), 0)
    col_id = lax.broadcasted_iota(jnp.int32, (heads, flat), 1)
    col_slot = jnp.where((col_id // slots) == row_id, col_id % slots, slots)
    places = [(j, b) for j in range(4) for b in range(rc)]

    def attend(i):
        for n_at, (j, b) in enumerate(places):
            at = j * quarter + i * rc + b
            q = qkv_ref[0, :, pl.ds(at, 1), :].reshape(heads, dim).astype(BF16)
            s = lax.dot_general(q, k_ref[at].reshape(flat, dim), (((1,), (1,)), ((), ())), preferred_element_type=F32)
            scores[n_at] = jnp.where(col_slot <= jnp.minimum(len_ref[at] - first, slots - 1), s * dim ** -0.5, NEG)
        s = scores[...]
        top = jnp.max(s, axis=2, keepdims=True)
        w = jnp.where(s > NEG, jnp.exp(s - top), 0.0)
        weight = jnp.sum(w, axis=2, keepdims=True)
        probs[...] = w.astype(BF16)
        for j in range(4):
            stat = jnp.zeros((heads, 128), F32)
            for b in range(rc):
                stat = jnp.where(lane == b, top[j * rc + b], stat)
                stat = jnp.where(lane == quarter + b, weight[j * rc + b], stat)
            st_ref[i, j] = stat
        for n_at, (j, b) in enumerate(places):
            at = j * quarter + i * rc + b
            acc_ref[at] = jnp.dot(probs[n_at], v_ref[at].reshape(flat, dim), preferred_element_type=F32)
        for k in range(2):
            a_stat(k, i).start()
            a_copy(k, i).start()

    def join_core(i):
        for k in range(2):
            a_stat(k, i).wait()
            a_copy(k, i).wait()
            packed, f_one, f_two, _ = join(st_ref[i, my_blocks[k]], got_st[k, i])
            for b in range(rc):
                at = i * rc + b
                value = acc_ref[my_blocks[k] * quarter + at] * f_one[:, b:b + 1] + got_acc[k, at] * f_two[:, b:b + 1]
                if k == 0:
                    fwd_acc[at] = value
                else:
                    own_acc[at] = value
            if k == 0:
                fwd_st[i] = packed
                b_stat(i).start()
                b_copy(i).start()
            else:
                own_st[i] = packed

    def join_chips(i):
        b_stat(i).wait()
        b_copy(i).wait()
        _, g_one, g_two, total = join(own_st[i], far_st[i])
        inv = 1.0 / jnp.where(lane < rc, total, 1.0)
        g_one = g_one * inv
        g_two = g_two * inv
        for b in range(rc):
            at = i * rc + b
            own_acc[at] = own_acc[at] * g_one[:, b:b + 1] + far_acc[at] * g_two[:, b:b + 1]
        for h in range(heads):
            att[i, :, pl.ds(h * dim, dim)] = own_acc[pl.ds(i * rc, rc), h, :].astype(BF16)

    col_tile = lambda j: pl.ds(pl.multiple_of(j * cc, cc), cc)

    def finish(value, block, k):
        rows = pl.ds(pl.multiple_of(block * quarter + (k // n_col) * rc, rc), rc)
        cols = col_tile(lax.rem(k, n_col))
        y_ref[rows, cols] = (x_buf[rows, cols].astype(F32) + value + b_ref[:, cols]).astype(BF16)

    def x_copy(k):
        return remote(mine.at[k], near.at[k], x_s.at[k], x_r.at[k], inward)

    def p_copy(k):
        return remote(half.at[k], far_half.at[k], p_s.at[k], p_r.at[k], peer)

    def t_copy(k):
        return remote(tot.at[k], tot.at[k], t_s.at[k], t_r.at[k], outward)

    def y_copy(k):
        return remote(tot.at[k], from_y.at[k], y_s.at[k], y_r.at[k], across)

    def c_copy(k):
        return remote(tot.at[k], from_c.at[k], c_s.at[k], c_r.at[k], mate)

    def f_copy(k):
        return remote(from_y.at[k], from_yc.at[k], f_s.at[k], f_r.at[k], mate)

    def x_arrives(k):
        return remote(mine.at[k], near.at[k], x_s.at[k], x_r.at[k], outward)

    def t_arrives(k):
        return remote(tot.at[k], tot.at[k], t_s.at[k], t_r.at[k], inward)

    def spread(k):
        y_copy(k).start()
        c_copy(k).start()
        finish(tot[k], r, k)

    def at_lag(k, lag, do):
        if isinstance(k, int):
            if 0 <= k - lag < n:
                do(k - lag)
        else:
            pl.when((k >= lag) & (k - lag < n))(lambda: do(k - lag))

    def relay(k):
        y_copy(k).wait_recv()
        f_copy(k).start()
        finish(from_y[k], (1 - chip_y) * 2 + core, k)

    def collect(k):
        c_copy(k).wait_recv()
        finish(from_c[k], chip_y * 2 + 1 - core, k)
        f_copy(k).wait_recv()
        finish(from_yc[k], (1 - chip_y) * 2 + 1 - core, k)

    def total_inner(k):
        p_copy(k).wait_recv()
        tot[k] = half[k] + far_half[k]
        t_copy(k).start()
        spread(k)

    def total_outer(k):
        t_arrives(k).wait_recv()
        spread(k)

    def half_inner(k):
        x_arrives(k).wait_recv()
        half[k] = mine[k] + near[k]
        p_copy(k).start()

    def after(k):
        @pl.when(outer)
        def _():
            at_lag(k, LAGS_OUTER[0], total_outer)
            at_lag(k, LAGS_OUTER[1], relay)
            at_lag(k, LAGS_OUTER[2], collect)

        @pl.when(jnp.logical_not(outer))
        def _():
            at_lag(k, LAG_HALF, half_inner)
            at_lag(k, LAGS_INNER[0], total_inner)
            at_lag(k, LAGS_INNER[1], relay)
            at_lag(k, LAGS_INNER[2], collect)

    @pl.loop(0, n_row + LAG_CHIPS)
    def _(i):
        @pl.when(i < n_row)
        def _():
            attend(i)

        @pl.when((i >= LAG_CORE) & (i - LAG_CORE < n_row))
        def _():
            join_core(i - LAG_CORE)

        @pl.when(i == LAG_CHIPS)
        def _():
            load_x.wait()
            for cp in w_loads:
                cp.wait()

        @pl.when(i >= LAG_CHIPS)
        def _():
            row = i - LAG_CHIPS
            join_chips(row)

            @pl.loop(0, n_col)
            def _(j):
                k = row * n_col + j
                mine[k] = jnp.dot(att[row], w_buf[:, col_tile(j)], preferred_element_type=F32)

                @pl.when(outer)
                def _():
                    x_copy(k).start()

                after(k)

    @pl.loop(n, n + max(LAGS_OUTER[2], LAGS_INNER[2]))
    def _(k):
        after(k)

    @pl.loop(0, n)
    def _(k):
        y_copy(k).wait_send()
        c_copy(k).wait_send()
        f_copy(k).wait_send()

        @pl.when(outer)
        def _():
            x_copy(k).wait_send()

        @pl.when(jnp.logical_not(outer))
        def _():
            p_copy(k).wait_send()
            t_copy(k).wait_send()


LAG_CORE = 1
LAG_CHIPS = 2
LAG_HALF = 2
LAGS_INNER = (5, 9, 11)
LAGS_OUTER = (16, 20, 22)


def combine(cache_len, qkv, k_new, v_new, tok_hidden, w_out, b_out, rc, cc):
    rows, heads, slots, dim = k_new.shape
    width = w_out.shape[1]
    quarter = rows // 4
    n_row, n_col = quarter // rc, width // cc
    n = n_row * n_col
    dma = pltpu.SemaphoreType.DMA
    part = pltpu.VMEM((quarter, heads, dim), F32)
    piece = pltpu.VMEM((n, rc, cc), F32)
    stat = pltpu.VMEM((n_row, heads, 128), F32)
    qkv, k_new, v_new = (pltpu.with_memory_space_constraint(a, pltpu.VMEM) for a in (qkv, k_new, v_new))
    vmem = pl.BlockSpec(memory_space=pltpu.VMEM)
    hbm = pl.BlockSpec(memory_space=pltpu.HBM)
    return pl.pallas_call(
        functools.partial(combine_kernel, quarter, rc, cc),
        in_specs=[hbm, vmem, vmem, vmem, hbm, hbm, hbm],
        out_specs=vmem,
        out_shape=pltpu.VMEM((rows, width), BF16),
        scratch_shapes=[
            pltpu.SMEM((rows,), jnp.int32), pltpu.VMEM(b_out.shape, BF16), pltpu.VMEM((1, width), F32),
            pltpu.VMEM((rows, heads, dim), F32), pltpu.VMEM((n_row, 4, heads, 128), F32),
            pltpu.VMEM((4 * rc, heads, heads * slots), F32), pltpu.VMEM((4 * rc, heads, heads * slots), BF16),
            pltpu.VMEM((2, quarter, heads, dim), F32), pltpu.VMEM((2, n_row, heads, 128), F32),
            part, stat, part, stat, part, stat,
            pltpu.VMEM((n_row, rc, heads * dim), BF16),
            pltpu.VMEM(w_out.shape, BF16), pltpu.VMEM((rows, width), BF16),
            *[piece] * 8,
            dma((1 + n_col,)), dma, dma,
            *[dma((2, n_row))] * 4,
            *[dma((n_row,))] * 4,
            *[dma((n,))] * 12,
        ],
        compiler_params=pltpu.CompilerParams(collective_id=0, has_side_effects=True, vmem_limit_bytes=30 * 2**20),
    )(*in_hbm(cache_len), qkv, k_new, v_new, *in_hbm(tok_hidden, w_out, b_out))


def solution(mesh):
    cache_spec = P('dp', 'tp', 'sp', None)
    row_spec = P('dp', None)

    def local_block(tok_hidden, cache_len, k_cache, v_cache, ln_gain, ln_bias, w_qkv, b_qkv, w_out, b_out):
        heads, dim, width = w_out.shape
        k_out, v_out, k_new, v_new, qkv = front(tok_hidden, cache_len, k_cache, v_cache, ln_gain, ln_bias, w_qkv, b_qkv, 2048, 3, 32)
        y = combine(cache_len, qkv, k_new, v_new, tok_hidden, w_out.reshape(heads * dim, width), b_out.reshape(width // 128, 128), 16, 1024)
        return y, k_out, v_out

    return jax.shard_map(
        local_block,
        mesh=mesh,
        in_specs=(row_spec, P('dp'), cache_spec, cache_spec, P(None), P(None), P(None, None, 'tp', None), P(None, 'tp', None), P('tp', None, None), P(None)),
        out_specs=(row_spec, cache_spec, cache_spec),
        check_vma=False,
    )
```

profile of v0, /device:TPU:1, one launch (start us, length us, event | category | flops | bytes accessed | tf_op | source)
XLA Modules:
  0.0 77.6 jit_solution(1054324554534860598)
XLA Ops:
  0.6 22.8 %shard_map.121 = (bf16[256,8,16,128]{3,2,1,0:T(8,128)(2,1)}, bf16[256,8,16,128]{3,2,1,0:T(8,128)(2,1)}, bf16[256,8,16,128]{3,2,1,0:T(8,128)(2,1)S(1)}, bf16[256,...) custom-call(s32[256]{0:T(256)} %len_hbm.3, bf16[256,4096]{1,0:T(8,128)(2,1)} %x_hbm.3, f32[1,4096]{1,0:T(1,128)} %bitcast.5, ...), custom_call_target="tpu_custom_call" | custom-call | tf_op jit(solution)/shard_map/pallas_call | solution.py:127
  23.5 52.8 %shard_map.122 = bf16[256,4096]{1,0:T(8,128)(2,1)S(1)} custom-call(s32[256]{0:T(256)} %len_hbm.3, f32[3,8,256,128]{3,2,1,0:T(8,128)S(1)} %get-tuple-element.8.qkv_ref, bf16[256,8,16,128]{3,2,1,0:T(8,128)(2,1)S(1)} %get-tuple-element.9.k_ref, bf16[256,8,16,128]{3,2,1,0:T(8,128)(2,1)S(1)} %get-tuple-element.10.v_ref, bf16[256,4096]{1,0:T(8,128)(2,1)} %x_hbm.3, ...), custom_call_target="tpu_custom_call" | custom-call | tf_op jit(solution)/shard_map/pallas_call | solution.py:447
  76.2 1.3 %copy.14 = bf16[256,4096]{1,0:T(8,128)(2,1)} copy(bf16[256,4096]{1,0:T(8,128)(2,1)S(1)} %shard_map.122) | data formatting | bytes 4194304
where the time goes:
time: 77.7 us; the launch traced here: 77.6 us
  Pallas kernels  75.6 us (97%)
  local copies, waits for them, and re-layouts  1.32 us (2%)
    pallas_call x1, Pallas kernels, combine(): pl.pallas_call(functools.partial(combine_kernel, quarter, rc, cc), in_spe...  52.8 us
    pallas_call x1, Pallas kernels, front(): pl.pallas_call(functools.partial(front_kernel, slots, mc, blk), in_specs=...  22.8 us

commit v1 on v0

--- a/solution.py
+++ b/solution.py
@@ -13,8 +13,39 @@
 BF16 = jnp.bfloat16
 
 
-def front_kernel(slots, mc, blk, len_hbm, x_hbm, gain_hbm, bias_hbm, w_hbm, bqkv_hbm, k_hbm, v_hbm,
-                 ko_hbm, vo_hbm, k_buf, v_buf, qkv, len_ref, gain_ref, bias_ref, bqkv_ref, x_buf, hid, w_buf,
+def attend_rows(places, row_at, slots, rc, len_ref, first, qkv_ref, k_ref, v_ref, scores, probs, put_stat, put_acc):
+    heads, dim = k_ref.shape[1], k_ref.shape[3]
+    flat = heads * slots
+    row_id = lax.broadcasted_iota(jnp.int32, (heads, flat), 0)
+    col_id = lax.broadcasted_iota(jnp.int32, (heads, flat), 1)
+    col_slot = jnp.where((col_id // slots) == row_id, col_id % slots, slots)
+    lane = lax.broadcasted_iota(jnp.int32, (heads, 128), 1)
+    for n_at, (j, b) in enumerate(places):
+        at = row_at(j, b)
+        q = qkv_ref[0, :, pl.ds(at, 1), :].reshape(heads, dim).astype(BF16)
+        s = lax.dot_general(q, k_ref[at].reshape(flat, dim), (((1,), (1,)), ((), ())), preferred_element_type=F32)
+        scores[n_at] = jnp.where(col_slot <= jnp.minimum(len_ref[at] - first, slots - 1), s * dim ** -0.5, NEG)
+    s = scores[...]
+    top = jnp.max(s, axis=2, keepdims=True)
+    w = jnp.where(s > NEG, jnp.exp(s - top), 0.0)
+    weight = jnp.sum(w, axis=2, keepdims=True)
+    probs[...] = w.astype(BF16)
+    for j in range(4):
+        m_tile = l_tile = jnp.zeros((heads, 128), F32)
+        for b in range(rc):
+            m_tile = jnp.where(lane == b, top[j * rc + b], m_tile)
+            l_tile = jnp.where(lane == b, weight[j * rc + b], l_tile)
+        put_stat(j, m_tile, l_tile)
+    for n_at, (j, b) in enumerate(places):
+        put_acc(j, b, jnp.dot(probs[n_at], v_ref[row_at(j, b)].reshape(flat, dim), preferred_element_type=F32))
+
+
+def places_of(rc):
+    return [(j, b) for j in range(4) for b in range(rc)]
+
+
+def front_kernel(slots, mc, blk, rc, len_hbm, x_hbm, gain_hbm, bias_hbm, w_hbm, bqkv_hbm, k_hbm, v_hbm,
+                 ko_hbm, vo_hbm, k_buf, v_buf, qkv, acc0, st0, scores, probs, len_ref, gain_ref, bias_ref, bqkv_ref, x_buf, hid, w_buf,
                  small_sem, x_sem, w_sem, k_sem, v_sem, ko_sem, vo_sem):
     rows, width = x_buf.shape
     heads, dim = qkv.shape[1], qkv.shape[3]
@@ -57,13 +88,6 @@
         centered = x - mean
         var = jnp.mean(centered * centered, axis=-1, keepdims=True)
         hid[part] = (centered * lax.rsqrt(var + 1e-5) * gain_ref[...] + bias_ref[...]).astype(BF16)
-        per = n_blk // EARLY
-
-        @pl.when(i < EARLY)
-        def _():
-            for u in range(per):
-                for cp in cache_copies(i * per + u):
-                    cp.start()
 
     @pl.loop(0, 3)
     def _(t):
@@ -88,6 +112,13 @@
             def _():
                 w_load(t + ahead // n_m, ahead % n_m, slot).start()
 
+            for at_chunk, (low, high) in enumerate(CACHE_PLAN):
+                @pl.when(c == at_chunk)
+                def _():
+                    for i in range(low * n_blk // 8, high * n_blk // 8):
+                        for cp in cache_copies(i):
+                            cp.start()
+
     slot_id = lax.broadcasted_iota(jnp.int32, (slots, dim), 0)
 
     @pl.loop(0, n_blk)
@@ -103,6 +134,17 @@
         for cp in out_copies(i):
             cp.start()
 
+    @pl.loop(0, acc0.shape[0])
+    def _(i):
+        def put_stat(j, m_tile, l_tile):
+            st0[i, j, 0] = m_tile
+            st0[i, j, 1] = l_tile
+
+        def put_acc(j, b, value):
+            acc0[i, j, b] = value
+
+        attend_rows(places_of(rc), lambda j, b: j * (rows // 4) + i * rc + b, slots, rc, len_ref, first, qkv, k_buf, v_buf, scores, probs, put_stat, put_acc)
+
     @pl.loop(0, n_blk)
     def _(i):
         for cp in out_copies(i):
@@ -110,14 +152,14 @@
 
 
 LN_ROWS = 64
-EARLY = 4
+CACHE_PLAN = ((0, 1), (1, 2), (2, 4), (4, 6), (6, 8))
 
 
 def in_hbm(*arrays):
     return [pltpu.with_memory_space_constraint(a, pltpu.HBM) for a in arrays]
 
 
-def front(tok_hidden, cache_len, k_cache, v_cache, ln_gain, ln_bias, w_qkv, b_qkv, mc, ring, blk):
+def front(tok_hidden, cache_len, k_cache, v_cache, ln_gain, ln_bias, w_qkv, b_qkv, mc, ring, blk, rc):
     rows, heads, slots, dim = k_cache.shape
     width = tok_hidden.shape[1]
     vmem = pl.BlockSpec(memory_space=pltpu.VMEM)
@@ -125,17 +167,20 @@
     dma = pltpu.SemaphoreType.DMA
     n_blk = rows // blk
     return pl.pallas_call(
-        functools.partial(front_kernel, slots, mc, blk),
+        functools.partial(front_kernel, slots, mc, blk, rc),
         in_specs=[hbm] * 8,
-        out_specs=[hbm, hbm, vmem, vmem, vmem],
+        out_specs=[hbm, hbm, vmem, vmem, vmem, vmem, vmem],
         out_shape=[
             jax.ShapeDtypeStruct(k_cache.shape, BF16),
             jax.ShapeDtypeStruct(v_cache.shape, BF16),
             pltpu.VMEM(k_cache.shape, BF16),
             pltpu.VMEM(v_cache.shape, BF16),
             pltpu.VMEM((3, heads, rows, dim), F32),
+            pltpu.VMEM((EARLY_CHUNKS, 4, rc, heads, dim), F32),
+            pltpu.VMEM((EARLY_CHUNKS, 4, 2, heads, 128), F32),
         ],
         scratch_shapes=[
+            pltpu.VMEM((4 * rc, heads, heads * slots), F32), pltpu.VMEM((4 * rc, heads, heads * slots), BF16),
             pltpu.SMEM((rows,), jnp.int32), pltpu.VMEM((1, width), F32), pltpu.VMEM((1, width), F32), pltpu.VMEM(b_qkv.shape, BF16),
             pltpu.VMEM((rows, width), BF16), pltpu.VMEM((rows, width), BF16),
             pltpu.VMEM((ring, mc, heads, dim), BF16),
@@ -145,7 +190,7 @@
     )(*in_hbm(cache_len, tok_hidden, ln_gain.reshape(1, width), ln_bias.reshape(1, width), w_qkv, b_qkv, k_cache, v_cache))
 
 
-def combine_kernel(quarter, rc, cc, len_hbm, qkv_ref, k_ref, v_ref, x_hbm, w_hbm, b_hbm, y_ref, len_ref, b_tiles, b_ref,
+def combine_kernel(quarter, rc, cc, len_hbm, qkv_ref, k_ref, v_ref, acc0, st0, x_hbm, w_hbm, b_hbm, y_ref, len_ref, b_tiles, b_ref,
                    acc_ref, st_ref, scores, probs, got_acc, got_st, fwd_acc, fwd_st, own_acc, own_st, far_acc, far_st, att,
                    w_buf, x_buf, mine, near, half, far_half, tot, from_y, from_c, from_yc, load_sem, len_sem, b_sem,
                    a_s, a_r, as_s, as_r, b_s, b_r, bs_s, bs_r,
@@ -175,6 +220,11 @@
         cp.start()
         w_loads.append(cp)
 
+    early = acc0.shape[0]
+    for i in range(early):
+        for j in range(4):
+            acc_ref[pl.ds(j * quarter + i * rc, rc)] = acc0[i, j]
+            st_ref[i, j] = st0[i, j]
     barrier = pltpu.get_barrier_semaphore()
     pl.semaphore_signal(barrier, inc=1, device_id=mate, device_id_type=MESH)
     pl.semaphore_signal(barrier, inc=1, device_id=across, device_id_type=MESH)
@@ -203,6 +253,13 @@
         return remote(acc_ref.at[pl.ds(mate_blocks[k] * quarter + i * rc, rc)], got_acc.at[k, pl.ds(i * rc, rc)],
                       a_s.at[k, i], a_r.at[k, i], mate)
 
+    def send_core(i):
+        for k in range(2):
+            a_stat(k, i).start()
+            a_copy(k, i).start()
+
+    for i in range(early):
+        send_core(i)
     load_len.wait()
     load_b.wait()
     bias = b_tiles[...].astype(F32)
@@ -211,14 +268,9 @@
     lane = lax.broadcasted_iota(jnp.int32, (heads, 128), 1)
 
     def join(one, two):
-        m_one, m_two = one, two
-        top = jnp.maximum(m_one, m_two)
-        f_one, f_two = jnp.exp(m_one - top), jnp.exp(m_two - top)
-        l_one = pltpu.roll(one, 128 - quarter, 1)
-        l_two = pltpu.roll(two, 128 - quarter, 1)
-        total = l_one * f_one + l_two * f_two
-        packed = jnp.where(lane < quarter, top, pltpu.roll(total, quarter, 1))
-        return packed, f_one, f_two, total
+        top = jnp.maximum(one[0], two[0])
+        f_one, f_two = jnp.exp(one[0] - top), jnp.exp(two[0] - top)
+        return top, one[1] * f_one + two[1] * f_two, f_one, f_two
 
     def b_stat(i):
         return remote(fwd_st.at[i], far_st.at[i], bs_s.at[i], bs_r.at[i], across)
@@ -227,41 +279,24 @@
         return remote(fwd_acc.at[pl.ds(i * rc, rc)], far_acc.at[pl.ds(i * rc, rc)], b_s.at[i], b_r.at[i], across)
 
     first = r * slots
-    flat = heads * slots
-    row_id = lax.broadcasted_iota(jnp.int32, (heads, flat), 0)
-    col_id = lax.broadcasted_iota(jnp.int32, (heads, flat), 1)
-    col_slot = jnp.where((col_id // slots) == row_id, col_id % slots, slots)
-    places = [(j, b) for j in range(4) for b in range(rc)]
-
     def attend(i):
-        for n_at, (j, b) in enumerate(places):
-            at = j * quarter + i * rc + b
-            q = qkv_ref[0, :, pl.ds(at, 1), :].reshape(heads, dim).astype(BF16)
-            s = lax.dot_general(q, k_ref[at].reshape(flat, dim), (((1,), (1,)), ((), ())), preferred_element_type=F32)
-            scores[n_at] = jnp.where(col_slot <= jnp.minimum(len_ref[at] - first, slots - 1), s * dim ** -0.5, NEG)
-        s = scores[...]
-        top = jnp.max(s, axis=2, keepdims=True)
-        w = jnp.where(s > NEG, jnp.exp(s - top), 0.0)
-        weight = jnp.sum(w, axis=2, keepdims=True)
-        probs[...] = w.astype(BF16)
-        for j in range(4):
-            stat = jnp.zeros((heads, 128), F32)
-            for b in range(rc):
-                stat = jnp.where(lane == b, top[j * rc + b], stat)
-                stat = jnp.where(lane == quarter + b, weight[j * rc + b], stat)
-            st_ref[i, j] = stat
-        for n_at, (j, b) in enumerate(places):
-            at = j * quarter + i * rc + b
-            acc_ref[at] = jnp.dot(probs[n_at], v_ref[at].reshape(flat, dim), preferred_element_type=F32)
-        for k in range(2):
-            a_stat(k, i).start()
-            a_copy(k, i).start()
+        row_at = lambda j, b: j * quarter + i * rc + b
+
+        def put_stat(j, m_tile, l_tile):
+            st_ref[i, j, 0] = m_tile
+            st_ref[i, j, 1] = l_tile
+
+        def put_acc(j, b, value):
+            acc_ref[row_at(j, b)] = value
+
+        attend_rows(places_of(rc), row_at, slots, rc, len_ref, first, qkv_ref, k_ref, v_ref, scores, probs, put_stat, put_acc)
+        send_core(i)
 
     def join_core(i):
         for k in range(2):
             a_stat(k, i).wait()
             a_copy(k, i).wait()
-            packed, f_one, f_two, _ = join(st_ref[i, my_blocks[k]], got_st[k, i])
+            top, total, f_one, f_two = join(st_ref[i, my_blocks[k]], got_st[k, i])
             for b in range(rc):
                 at = i * rc + b
                 value = acc_ref[my_blocks[k] * quarter + at] * f_one[:, b:b + 1] + got_acc[k, at] * f_two[:, b:b + 1]
@@ -270,16 +305,18 @@
                 else:
                     own_acc[at] = value
             if k == 0:
-                fwd_st[i] = packed
+                fwd_st[i, 0] = top
+                fwd_st[i, 1] = total
                 b_stat(i).start()
                 b_copy(i).start()
             else:
-                own_st[i] = packed
+                own_st[i, 0] = top
+                own_st[i, 1] = total
 
     def join_chips(i):
         b_stat(i).wait()
         b_copy(i).wait()
-        _, g_one, g_two, total = join(own_st[i], far_st[i])
+        _, total, g_one, g_two = join(own_st[i], far_st[i])
         inv = 1.0 / jnp.where(lane < rc, total, 1.0)
         g_one = g_one * inv
         g_two = g_two * inv
@@ -372,37 +409,41 @@
             at_lag(k, LAGS_INNER[1], relay)
             at_lag(k, LAGS_INNER[2], collect)
 
-    @pl.loop(0, n_row + LAG_CHIPS)
-    def _(i):
-        @pl.when(i < n_row)
-        def _():
-            attend(i)
-
-        @pl.when((i >= LAG_CORE) & (i - LAG_CORE < n_row))
-        def _():
-            join_core(i - LAG_CORE)
-
-        @pl.when(i == LAG_CHIPS)
-        def _():
-            load_x.wait()
-            for cp in w_loads:
-                cp.wait()
-
-        @pl.when(i >= LAG_CHIPS)
-        def _():
-            row = i - LAG_CHIPS
-            join_chips(row)
-
-            @pl.loop(0, n_col)
-            def _(j):
-                k = row * n_col + j
-                mine[k] = jnp.dot(att[row], w_buf[:, col_tile(j)], preferred_element_type=F32)
-
-                @pl.when(outer)
-                def _():
-                    x_copy(k).start()
-
-                after(k)
+    @pl.loop(0, early)
+    def _(i):
+        join_core(i)
+
+    @pl.loop(early, min(early + 1, n_row))
+    def _(i):
+        attend(i)
+
+    load_x.wait()
+    for cp in w_loads:
+        cp.wait()
+
+    @pl.loop(early + 1, n_row)
+    def _(i):
+        attend(i)
+
+    @pl.loop(early, n_row)
+    def _(i):
+        join_core(i)
+
+    @pl.loop(0, n_row)
+    def _(row):
+        join_chips(row)
+
+        @pl.loop(0, n_col)
+        def _(j):
+            k = row * n_col + j
+            mine[k] = jnp.dot(att[row], w_buf[:, col_tile(j)], preferred_element_type=F32)
+
+            @pl.when(outer)
+            def _():
+                x_copy(k).start()
+
+            after(k)
+
 
     @pl.loop(n, n + max(LAGS_OUTER[2], LAGS_INNER[2]))
     def _(k):
@@ -424,14 +465,15 @@
             t_copy(k).wait_send()
 
 
-LAG_CORE = 1
-LAG_CHIPS = 2
+ROWS = 16
+COLS = 1024
 LAG_HALF = 2
-LAGS_INNER = (5, 9, 11)
+EARLY_CHUNKS = 3
+LAGS_INNER = (5, 8, 10)
 LAGS_OUTER = (16, 20, 22)
 
 
-def combine(cache_len, qkv, k_new, v_new, tok_hidden, w_out, b_out, rc, cc):
+def combine(cache_len, qkv, k_new, v_new, acc0, st0, tok_hidden, w_out, b_out, rc, cc):
     rows, heads, slots, dim = k_new.shape
     width = w_out.shape[1]
     quarter = rows // 4
@@ -440,20 +482,20 @@
     dma = pltpu.SemaphoreType.DMA
     part = pltpu.VMEM((quarter, heads, dim), F32)
     piece = pltpu.VMEM((n, rc, cc), F32)
-    stat = pltpu.VMEM((n_row, heads, 128), F32)
-    qkv, k_new, v_new = (pltpu.with_memory_space_constraint(a, pltpu.VMEM) for a in (qkv, k_new, v_new))
+    stat = pltpu.VMEM((n_row, 2, heads, 128), F32)
+    made = [pltpu.with_memory_space_constraint(a, pltpu.VMEM) for a in (qkv, k_new, v_new, acc0, st0)]
     vmem = pl.BlockSpec(memory_space=pltpu.VMEM)
     hbm = pl.BlockSpec(memory_space=pltpu.HBM)
     return pl.pallas_call(
         functools.partial(combine_kernel, quarter, rc, cc),
-        in_specs=[hbm, vmem, vmem, vmem, hbm, hbm, hbm],
+        in_specs=[hbm, vmem, vmem, vmem, vmem, vmem, hbm, hbm, hbm],
         out_specs=vmem,
         out_shape=pltpu.VMEM((rows, width), BF16),
         scratch_shapes=[
             pltpu.SMEM((rows,), jnp.int32), pltpu.VMEM(b_out.shape, BF16), pltpu.VMEM((1, width), F32),
-            pltpu.VMEM((rows, heads, dim), F32), pltpu.VMEM((n_row, 4, heads, 128), F32),
+            pltpu.VMEM((rows, heads, dim), F32), pltpu.VMEM((n_row, 4, 2, heads, 128), F32),
             pltpu.VMEM((4 * rc, heads, heads * slots), F32), pltpu.VMEM((4 * rc, heads, heads * slots), BF16),
-            pltpu.VMEM((2, quarter, heads, dim), F32), pltpu.VMEM((2, n_row, heads, 128), F32),
+            pltpu.VMEM((2, quarter, heads, dim), F32), pltpu.VMEM((2, n_row, 2, heads, 128), F32),
             part, stat, part, stat, part, stat,
             pltpu.VMEM((n_row, rc, heads * dim), BF16),
             pltpu.VMEM(w_out.shape, BF16), pltpu.VMEM((rows, width), BF16),
@@ -464,7 +506,7 @@
             *[dma((n,))] * 12,
         ],
         compiler_params=pltpu.CompilerParams(collective_id=0, has_side_effects=True, vmem_limit_bytes=30 * 2**20),
-    )(*in_hbm(cache_len), qkv, k_new, v_new, *in_hbm(tok_hidden, w_out, b_out))
+    )(*in_hbm(cache_len), *made, *in_hbm(tok_hidden, w_out, b_out))
 
 
 def solution(mesh):
@@ -473,8 +515,10 @@
 
     def local_block(tok_hidden, cache_len, k_cache, v_cache, ln_gain, ln_bias, w_qkv, b_qkv, w_out, b_out):
         heads, dim, width = w_out.shape
-        k_out, v_out, k_new, v_new, qkv = front(tok_hidden, cache_len, k_cache, v_cache, ln_gain, ln_bias, w_qkv, b_qkv, 2048, 3, 32)
-        y = combine(cache_len, qkv, k_new, v_new, tok_hidden, w_out.reshape(heads * dim, width), b_out.reshape(width // 128, 128), 16, 1024)
+        k_out, v_out, *parts, acc0, st0 = front(tok_hidden, cache_len, k_cache, v_cache, ln_gain, ln_bias, w_qkv, b_qkv, 2048, 3, 32, ROWS)
+        k_new, v_new, qkv = parts
+        y = combine(cache_len, qkv, k_new, v_new, acc0, st0, tok_hidden, w_out.reshape(heads * dim, width),
+                    b_out.reshape(width // 128, 128), ROWS, COLS)
         return y, k_out, v_out
 
     return jax.shard_map(

time: 77.7 us -> 75.8 us (0.976)
  Pallas kernels: 75.6 us -> 73.7 us
    pallas_call x1, Pallas kernels: 52.8 us -> 49.4 us  [combine(): pl.pallas_call(functools.partial(combine_kernel, quarter, rc, cc), in_spe...]
    pallas_call x1, Pallas kernels: 22.8 us -> 24.3 us  [front(): pl.pallas_call(functools.partial(front_kernel, slots, mc, blk, rc), in_sp...]
where the time goes in v1:
time: 75.8 us; the launch traced here: 75.7 us
  Pallas kernels  73.7 us (97%)
  local copies, waits for them, and re-layouts  1.32 us (2%)
    pallas_call x1, Pallas kernels, combine(): pl.pallas_call(functools.partial(combine_kernel, quarter, rc, cc), in_spe...  49.4 us
    pallas_call x1, Pallas kernels, front(): pl.pallas_call(functools.partial(front_kernel, slots, mc, blk, rc), in_sp...  24.3 us

profile of v1, /device:TPU:1, one launch (start us, length us, event | category | flops | bytes accessed | tf_op | source)
XLA Modules:
  0.0 75.7 jit_solution(4165450519312277323)
XLA Ops:
  0.6 24.3 %shard_map.121 = (bf16[256,8,16,128]{3,2,1,0:T(8,128)(2,1)}, bf16[256,8,16,128]{3,2,1,0:T(8,128)(2,1)}, bf16[256,8,16,128]{3,2,1,0:T(8,128)(2,1)S(1)}, bf16[256,...) custom-call(s32[256]{0:T(256)} %len_hbm.3, ...), custom_call_target="tpu_custom_call" | custom-call | tf_op jit(solution)/shard_map/pallas_call | solution.py:169
  24.9 49.4 %shard_map.122 = bf16[256,4096]{1,0:T(8,128)(2,1)S(1)} custom-call(s32[256]{0:T(256)} %len_hbm.3, f32[3,8,256,128]{3,2,1,0:T(8,128)S(1)} %get-tuple-element.10.qkv_ref, bf16[256,8,16,128]{3,2,1,0:T(8,128)(2,1)S(1)} %get-tuple-element.11.k_ref, bf16[256,8,16,128]{3,2,1,0:T(8,128)(2,1)S(1)} %get-tuple-element.12.v_ref, ...), custom_call_target="tpu_custom_call" | custom-call | tf_op jit(solution)/shard_map/pallas_call | solution.py:489
  74.3 1.3 %copy.14 = bf16[256,4096]{1,0:T(8,128)(2,1)} copy(bf16[256,4096]{1,0:T(8,128)(2,1)S(1)} %shard_map.122) | data formatting | bytes 4194304
